TPU v7x, 32 devices: a whole 2x2x4 slice. The times are simulated.
32 devices in a mesh: reps: 2 (over x), grow: 16 (over z, y, core).
Axes of the slice: x: 2, y: 2, z: 4, core: 2. Of those that a mesh axis runs over, the one named last changes fastest.
Arguments:
- hamiltonian: float32 [192, 3, 256, 256], P(('reps', 'grow')), parts along dimension 0, may hold values from -3 to 3, as said below
- pattern: int32 [96, 3], replicated, may hold values from 0 to 1, as said below
- potential: float32 [2], P('reps'), parts along dimension 0, may hold values from -0.2 to 0.2
Outputs:
- sign_matrix: float32 [192, 3, 256, 256], P(('reps', 'grow')), parts along dimension 0
- occupation: float32 [2], P('reps'), parts along dimension 0
There are 2 independent parts, one for each index of `reps`. A program takes and returns all parts, laid end to end along the dimension named above; an argument that names none is the same for every part. Nothing has to cross between parts.
Inputs may be any that keep to these rules, and one draw needn't show every extreme that they name: `hamiltonian`: the matrix is symmetric: slot 2 of block row i is the transpose of slot 0 of block row i + 1, slot 1 is symmetric, slot 0 of row 0 and slot 2 of row 95 are zero. pattern[i, 1] = 1; pattern[i, 2] = pattern[i + 1, 0]; pattern[0, 0] = pattern[95, 2] = 0.
All inputs are finite; a program needn't handle non-finite values.
Results may differ from a plain program's by a relative error of at most 0.0001.
Values sent between devices are 32-bit elements; how exact they have to be, the bound alone decides.
A program may use at most 64 MiB of HBM per device.

v0:
```python
import functools

import jax
import jax.numpy as jnp
from jax import lax
from jax.experimental import pallas as pl
from jax.experimental.pallas import tpu as pltpu
from jax.sharding import PartitionSpec as P

F32 = jnp.float32
BF16 = jnp.bfloat16
PIECES = 4
MESH = pl.DeviceIdType.MESH


def product(left, right, left_at, right_at, transposed=False):
    (lh, ll), (rh, rl) = left, right
    dims = (((1,), (1 if transposed else 0,)), ((), ()))

    def dot(a, b):
        return lax.dot_general(a, b, dims, preferred_element_type=F32)

    a_hi, a_lo, b_hi, b_lo = lh[left_at], ll[left_at], rh[right_at], rl[right_at]
    return (dot(a_lo, b_hi) + dot(a_hi, b_lo)) + dot(a_hi, b_hi)


def store(pair, at, value):
    high = value.astype(BF16)
    pair[0][at] = high
    pair[1][at] = (value - high.astype(F32)).astype(BF16)


def kernel(n, h, pattern, potential, out, occupation, *scratch):
    (stage, result, before, after, parts, trace_tile, ah, al, sh, sl, crh, crl, cch, ccl, s2h, s2l,
     load_sem, store_sem, next_send, next_recv, prev_send, prev_recv, part_send, part_recv) = scratch
    rows, edge = h.shape[0], h.shape[2]
    row_total = pattern.shape[0]
    me = lax.axis_index("grow")
    has_prev, has_next = me > 0, me < n - 1
    a, s, cr, cc, s2 = (ah, al), (sh, sl), (crh, crl), (cch, ccl), (s2h, s2l)

    loads = [pltpu.make_async_copy(h.at[r], stage.at[r], load_sem.at[r]) for r in range(rows)]
    for load in loads:
        load.start()

    barrier = pltpu.get_barrier_semaphore()

    @pl.loop(1, n)
    def _(k):
        pl.semaphore_signal(barrier, inc=1, device_id={"grow": lax.rem(me + k, n)}, device_id_type=MESH)

    pl.semaphore_wait(barrier, n - 1)

    last = rows - 1
    to_next = [
        pltpu.make_async_remote_copy(
            src_ref=h.at[r, c], dst_ref=before.at[p], send_sem=next_send.at[p], recv_sem=next_recv.at[p],
            device_id={"grow": lax.rem(me + 1, n)}, device_id_type=MESH)
        for p, (r, c) in enumerate([(last, 1), (last, 0), (last - 1, 1), (last - 1, 0)])
    ]
    to_prev = [
        pltpu.make_async_remote_copy(
            src_ref=h.at[r, c], dst_ref=after.at[p], send_sem=prev_send.at[p], recv_sem=prev_recv.at[p],
            device_id={"grow": lax.rem(me + n - 1, n)}, device_id_type=MESH)
        for p, (r, c) in enumerate([(0, 1), (0, 2), (1, 1), (1, 2)])
    ]

    @pl.when(has_next)
    def _():
        for copy in to_next:
            copy.start()

    @pl.when(has_prev)
    def _():
        for copy in to_prev:
            copy.start()

    @pl.when(jnp.logical_not(has_prev))
    def _():
        before[...] = jnp.zeros_like(before)

    @pl.when(jnp.logical_not(has_next))
    def _():
        after[...] = jnp.zeros_like(after)

    def arrive(p):
        @pl.when(has_prev)
        def _():
            to_next[p].wait_recv()

        @pl.when(has_next)
        def _():
            to_prev[p].wait_recv()

    def on_diagonal():
        return lax.broadcasted_iota(jnp.int32, (edge, edge), 0) == lax.broadcasted_iota(
            jnp.int32, (edge, edge), 1)

    def mask(e, c):
        row = jnp.clip(me * rows + e - 2, 0, row_total - 1)
        return pattern[row, c].astype(F32)

    def lanes(c):
        return slice(c * edge, (c + 1) * edge)

    def put_a(e, c, block):
        value = -block
        if c == 1:
            value = jnp.where(on_diagonal(), potential[0] + value, value)
        store(a, (e, slice(None), lanes(c)), value * mask(e, c))

    left_of = {0: slice(0, 2 * edge), 1: slice(0, 3 * edge), 2: slice(edge, 3 * edge)}
    right_of = {0: slice(edge, 3 * edge), 1: slice(0, 3 * edge), 2: slice(0, 2 * edge)}
    full = slice(None)

    def filtered(left, right, e, c, transposed=False):
        right_at = (e + c - 1, full, right_of[c]) if transposed else (e + c - 1, right_of[c], full)
        return product(left, right, (e, full, left_of[c]), right_at, transposed)

    def shifted(square, e, c):
        value = -square
        if c == 1:
            value = jnp.where(on_diagonal(), 3.0 + value, value)
        return value * mask(e, c)

    def column_at(e, c):
        return (e + c - 1, lanes(2 - c), full)

    def f1(e, slots=(0, 1, 2)):
        for c in slots:
            store(s, column_at(e, c), shifted(filtered(a, a, e, c, True), e, c))

    def f2(e, slots=(0, 1, 2)):
        for c in slots:
            value = filtered(a, s, e, c) * (0.5 * mask(e, c))
            store(cr, (e, full, lanes(c)), value)
            store(cc, column_at(e, c), value)

    def f3(e, slots=(0, 1, 2)):
        for c in slots:
            store(s2, column_at(e, c), shifted(filtered(cr, cc, e, c), e, c))

    def f4(e):
        for c in range(3):
            value = filtered(cr, s2, e, c) * (0.5 * mask(e, c))
            result[e - 2, c] = value
            if c == 1:
                trace_tile[...] += jnp.sum(jnp.where(on_diagonal(), value, 0.0), axis=0, keepdims=True)
        pltpu.make_async_copy(result.at[e - 2], out.at[e - 2], store_sem.at[e - 2]).start()

    def span(function, low, high):
        pl.loop(low, high)(function)

    def both(function, low, high):
        @pl.loop(0, 2)
        def _(k):
            function(low + k * (high - low))

    trace_tile[...] = jnp.zeros_like(trace_tile)
    lo, hi = 2, rows + 1
    for r in range(rows):
        loads[r].wait()
        for c in range(3):
            put_a(r + 2, c, stage[r, c])
    span(f1, lo + 1, hi)
    span(f2, lo + 2, hi - 1)

    put_a(lo - 1, 2, stage[0, 0].T)
    put_a(hi + 1, 0, stage[last, 2].T)
    arrive(0)
    put_a(lo - 1, 1, before[0])
    put_a(hi + 1, 1, after[0])
    both(f1, lo, hi)
    both(f2, lo + 1, hi - 1)
    span(f3, lo + 2, hi - 1)

    arrive(1)
    put_a(lo - 1, 0, before[1])
    put_a(lo - 2, 2, before[1].T)
    put_a(hi + 1, 2, after[1])
    put_a(hi + 2, 0, after[1].T)
    f1(lo - 1, (1, 2))
    f1(hi + 1, (0, 1))
    both(f2, lo, hi)
    both(f3, lo + 1, hi - 1)
    span(f4, lo + 2, hi - 1)

    arrive(2)
    put_a(lo - 2, 1, before[2])
    put_a(hi + 2, 1, after[2])
    f1(lo - 1, (0,))
    f1(lo - 2, (2,))
    f1(hi + 1, (2,))
    f1(hi + 2, (0,))
    f2(lo - 1, (1, 2))
    f2(hi + 1, (0, 1))
    both(f3, lo, hi)
    f3(lo - 1, (2,))
    f3(hi + 1, (0,))
    both(f4, lo + 1, hi - 1)

    arrive(3)
    put_a(lo - 2, 0, before[3])
    put_a(hi + 2, 2, after[3])
    f1(lo - 2, (1,))
    f1(hi + 2, (1,))
    f2(lo - 1, (0,))
    f2(lo - 2, (2,))
    f2(hi + 1, (2,))
    f2(hi + 2, (0,))
    f3(lo - 1, (1,))
    f3(hi + 1, (1,))
    both(f4, lo, hi)

    parts[me] = jnp.broadcast_to(trace_tile[...], parts.shape[1:])

    def part_copy(target, slot):
        return pltpu.make_async_remote_copy(
            src_ref=parts.at[me], dst_ref=parts.at[me], send_sem=part_send.at[target],
            recv_sem=part_recv.at[slot], device_id={"grow": target}, device_id_type=MESH)

    @pl.loop(1, n)
    def _(k):
        part_copy(lax.rem(me + k, n), me).start()

    for r in range(rows):
        pltpu.make_async_copy(result.at[r], out.at[r], store_sem.at[r]).wait()

    @pl.when(has_next)
    def _():
        for copy in to_next:
            copy.wait_send()

    @pl.when(has_prev)
    def _():
        for copy in to_prev:
            copy.wait_send()

    @pl.loop(1, n)
    def _(k):
        other = lax.rem(me + k, n)
        copy = part_copy(other, other)
        copy.wait_recv()
        copy.wait_send()

    order = float(row_total * edge)
    total = jnp.sum(jnp.sum(parts[...], axis=0)[0:1])
    occupation[0] = (order + total) / (2.0 * order)


def local(n, hamiltonian, pattern, potential):
    rows, edge = hamiltonian.shape[0], hamiltonian.shape[2]
    wide, tall = (rows + 4, edge, 3 * edge), (rows + 4, 3 * edge, edge)
    pairs = [wide, tall, wide, tall, tall]
    any_space = pl.BlockSpec(memory_space=pl.ANY)
    scalars = pl.BlockSpec(memory_space=pltpu.SMEM)
    sems = pltpu.SemaphoreType.DMA
    return pl.pallas_call(
        functools.partial(kernel, n),
        out_shape=(jax.ShapeDtypeStruct(hamiltonian.shape, F32), jax.ShapeDtypeStruct((1,), F32)),
        in_specs=[any_space, scalars, scalars],
        out_specs=(any_space, scalars),
        scratch_shapes=[
            pltpu.VMEM((rows, 3, edge, edge), F32),
            pltpu.VMEM((rows, 3, edge, edge), F32),
            pltpu.VMEM((PIECES, edge, edge), F32),
            pltpu.VMEM((PIECES, edge, edge), F32),
            pltpu.VMEM((n, 8, edge), F32),
            pltpu.VMEM((1, edge), F32),
            *[pltpu.VMEM(shape, BF16) for shape in pairs for _ in range(2)],
            sems((rows,)), sems((rows,)), sems((PIECES,)), sems((PIECES,)), sems((PIECES,)), sems((PIECES,)),
            sems((n,)), sems((n,)),
        ],
        compiler_params=pltpu.CompilerParams(
            collective_id=0, has_side_effects=True, vmem_limit_bytes=62 * 1024 * 1024),
        name="sign_iterations",
    )(hamiltonian, pattern, potential)


def solution(mesh):
    in_specs = (P(("reps", "grow"), None, None, None), P(), P("reps"))
    out_specs = (P(("reps", "grow"), None, None, None), P("reps"))
    return jax.shard_map(
        functools.partial(local, mesh.shape["grow"]),
        mesh=mesh, in_specs=in_specs, out_specs=out_specs, check_vma=False)
```

profile of v0, /device:TPU:0, one launch (start us, length us, event | category | flops | bytes accessed | tf_op | source)
XLA Modules:
  0.0 60.7 jit_solution(16379153579680800316)
XLA Ops:
  1.3 1.4 %copy.5.pattern = s32[96,3]{1,0:T(8,128)} copy(s32[96,3]{0,1:T(4,128)} %param.4) | data formatting | bytes 2304 | tf_op args[1]
  2.7 51.3 %sign_iterations.1 = (f32[6,3,256,256]{3,2,1,0:T(8,128)}, f32[1]{0:T(128)}) custom-call(f32[6,3,256,256]{3,2,1,0:T(8,128)} %h.1, s32[96,3]{1,0:T(8,128)} %copy.5.pattern, f32[1]{0:T(128)S(6)} %copy.8.potential), custom_call_target="tpu_custom_call" | custom-call | tf_op jit(solution)/shard_map/sign_iterations/pallas_call | solution.py:258
  54.0 4.9 %copy.9 = f32[6,3,256,256]{3,2,1,0:T(8,128)} copy(f32[6,3,256,256]{3,2,1,0:T(8,128)} %get-tuple-element.4) | data formatting | bytes 9437184
where the time goes:
time: 61 us; the launch traced here: 60.7 us
  Pallas kernels  51.3 us (84%)
  local copies, waits for them, and re-layouts  6.33 us (10%)
  between operations  3.05 us (5%)
    pallas_call x1, Pallas kernels, local(): pl.pallas_call(functools.partial(kernel, n), out_shape=(jax.ShapeDtypeStr...  51.3 us
    unnamed x2, local copies, waits for them, and re-layouts  6.33 us

commit v1 on v0

--- a/solution.py
+++ b/solution.py
@@ -10,6 +10,7 @@
 F32 = jnp.float32
 BF16 = jnp.bfloat16
 PIECES = 4
+VMEM_LIMIT = 50 * 1024 * 1024
 MESH = pl.DeviceIdType.MESH
 
 
@@ -31,10 +32,10 @@
 
 
 def kernel(n, h, pattern, potential, out, occupation, *scratch):
-    (stage, result, before, after, parts, trace_tile, ah, al, sh, sl, crh, crl, cch, ccl, s2h, s2l,
-     load_sem, store_sem, next_send, next_recv, prev_send, prev_recv, part_send, part_recv) = scratch
+    (stage, before, after, parts, trace_tile, ah, al, sh, sl, crh, crl, cch, ccl, s2h, s2l,
+     load_sem, next_send, next_recv, prev_send, prev_recv, part_send, part_recv) = scratch
     rows, edge = h.shape[0], h.shape[2]
-    row_total = pattern.shape[0]
+    row_total = pattern.shape[1]
     me = lax.axis_index("grow")
     has_prev, has_next = me > 0, me < n - 1
     a, s, cr, cc, s2 = (ah, al), (sh, sl), (crh, crl), (cch, ccl), (s2h, s2l)
@@ -98,7 +99,7 @@
 
     def mask(e, c):
         row = jnp.clip(me * rows + e - 2, 0, row_total - 1)
-        return pattern[row, c].astype(F32)
+        return pattern[c, row].astype(F32)
 
     def lanes(c):
         return slice(c * edge, (c + 1) * edge)
@@ -126,9 +127,17 @@
     def column_at(e, c):
         return (e + c - 1, lanes(2 - c), full)
 
-    def f1(e, slots=(0, 1, 2)):
-        for c in slots:
-            store(s, column_at(e, c), shifted(filtered(a, a, e, c, True), e, c))
+    def diagonal(e):
+        high, low = ah[e], al[e]
+        dims = (((1,), (1,)), ((), ()))
+        cross = lax.dot_general(high, low, dims, preferred_element_type=F32)
+        square = lax.dot_general(high, high, dims, preferred_element_type=F32)
+        store(s, column_at(e, 1), shifted((cross + cross.T) + square, e, 1))
+
+    def upper(e):
+        value = shifted(filtered(a, a, e, 2, True), e, 2)
+        store(s, column_at(e, 2), value)
+        store(s, column_at(e + 1, 0), value.T)
 
     def f2(e, slots=(0, 1, 2)):
         for c in slots:
@@ -140,13 +149,12 @@
         for c in slots:
             store(s2, column_at(e, c), shifted(filtered(cr, cc, e, c), e, c))
 
-    def f4(e):
-        for c in range(3):
+    def f4(e, slots=(0, 1, 2)):
+        for c in slots:
             value = filtered(cr, s2, e, c) * (0.5 * mask(e, c))
-            result[e - 2, c] = value
+            out[e - 2, c] = value
             if c == 1:
                 trace_tile[...] += jnp.sum(jnp.where(on_diagonal(), value, 0.0), axis=0, keepdims=True)
-        pltpu.make_async_copy(result.at[e - 2], out.at[e - 2], store_sem.at[e - 2]).start()
 
     def span(function, low, high):
         pl.loop(low, high)(function)
@@ -162,55 +170,48 @@
         loads[r].wait()
         for c in range(3):
             put_a(r + 2, c, stage[r, c])
-    span(f1, lo + 1, hi)
-    span(f2, lo + 2, hi - 1)
+    span(diagonal, lo, hi + 1)
+    span(upper, lo, hi)
+    span(f2, lo + 1, hi)
+    span(f3, lo + 2, hi - 1)
 
     put_a(lo - 1, 2, stage[0, 0].T)
     put_a(hi + 1, 0, stage[last, 2].T)
     arrive(0)
     put_a(lo - 1, 1, before[0])
     put_a(hi + 1, 1, after[0])
-    both(f1, lo, hi)
-    both(f2, lo + 1, hi - 1)
-    span(f3, lo + 2, hi - 1)
+    both(upper, lo - 1, hi)
+    f2(lo, (1, 2))
+    f2(hi, (0, 1))
+    f2(lo - 1, (2,))
+    f2(hi + 1, (0,))
+    both(f3, lo + 1, hi - 1)
+    span(f4, lo + 2, hi - 1)
 
     arrive(1)
     put_a(lo - 1, 0, before[1])
     put_a(lo - 2, 2, before[1].T)
     put_a(hi + 1, 2, after[1])
     put_a(hi + 2, 0, after[1].T)
-    f1(lo - 1, (1, 2))
-    f1(hi + 1, (0, 1))
-    both(f2, lo, hi)
-    both(f3, lo + 1, hi - 1)
-    span(f4, lo + 2, hi - 1)
+    both(diagonal, lo - 1, hi + 1)
+    f2(lo, (0,))
+    f2(hi, (2,))
+    f3(lo, (1, 2))
+    f3(hi, (0, 1))
+    both(f4, lo + 1, hi - 1)
 
     arrive(2)
     put_a(lo - 2, 1, before[2])
     put_a(hi + 2, 1, after[2])
-    f1(lo - 1, (0,))
-    f1(lo - 2, (2,))
-    f1(hi + 1, (2,))
-    f1(hi + 2, (0,))
-    f2(lo - 1, (1, 2))
-    f2(hi + 1, (0, 1))
-    both(f3, lo, hi)
+    both(upper, lo - 2, hi + 1)
+    f2(lo - 1, (1,))
+    f2(hi + 1, (1,))
+    f3(lo, (0,))
+    f3(hi, (2,))
     f3(lo - 1, (2,))
     f3(hi + 1, (0,))
-    both(f4, lo + 1, hi - 1)
-
-    arrive(3)
-    put_a(lo - 2, 0, before[3])
-    put_a(hi + 2, 2, after[3])
-    f1(lo - 2, (1,))
-    f1(hi + 2, (1,))
-    f2(lo - 1, (0,))
-    f2(lo - 2, (2,))
-    f2(hi + 1, (2,))
-    f2(hi + 2, (0,))
-    f3(lo - 1, (1,))
-    f3(hi + 1, (1,))
-    both(f4, lo, hi)
+    f4(lo, (1, 2))
+    f4(hi, (0, 1))
 
     parts[me] = jnp.broadcast_to(trace_tile[...], parts.shape[1:])
 
@@ -223,8 +224,18 @@
     def _(k):
         part_copy(lax.rem(me + k, n), me).start()
 
-    for r in range(rows):
-        pltpu.make_async_copy(result.at[r], out.at[r], store_sem.at[r]).wait()
+    arrive(3)
+    put_a(lo - 2, 0, before[3])
+    put_a(hi + 2, 2, after[3])
+    both(diagonal, lo - 2, hi + 2)
+    f2(lo - 1, (0,))
+    f2(hi + 1, (2,))
+    f2(lo - 2, (2,))
+    f2(hi + 2, (0,))
+    f3(lo - 1, (1,))
+    f3(hi + 1, (1,))
+    f4(lo, (0,))
+    f4(hi, (2,))
 
     @pl.when(has_next)
     def _():
@@ -257,24 +268,23 @@
     sems = pltpu.SemaphoreType.DMA
     return pl.pallas_call(
         functools.partial(kernel, n),
-        out_shape=(jax.ShapeDtypeStruct(hamiltonian.shape, F32), jax.ShapeDtypeStruct((1,), F32)),
+        out_shape=(pltpu.VMEM(hamiltonian.shape, F32), jax.ShapeDtypeStruct((1,), F32)),
         in_specs=[any_space, scalars, scalars],
-        out_specs=(any_space, scalars),
+        out_specs=(pl.BlockSpec(memory_space=pltpu.VMEM), scalars),
         scratch_shapes=[
-            pltpu.VMEM((rows, 3, edge, edge), F32),
             pltpu.VMEM((rows, 3, edge, edge), F32),
             pltpu.VMEM((PIECES, edge, edge), F32),
             pltpu.VMEM((PIECES, edge, edge), F32),
             pltpu.VMEM((n, 8, edge), F32),
             pltpu.VMEM((1, edge), F32),
             *[pltpu.VMEM(shape, BF16) for shape in pairs for _ in range(2)],
-            sems((rows,)), sems((rows,)), sems((PIECES,)), sems((PIECES,)), sems((PIECES,)), sems((PIECES,)),
+            sems((rows,)), sems((PIECES,)), sems((PIECES,)), sems((PIECES,)), sems((PIECES,)),
             sems((n,)), sems((n,)),
         ],
         compiler_params=pltpu.CompilerParams(
-            collective_id=0, has_side_effects=True, vmem_limit_bytes=62 * 1024 * 1024),
+            collective_id=0, has_side_effects=True, vmem_limit_bytes=VMEM_LIMIT),
         name="sign_iterations",
-    )(hamiltonian, pattern, potential)
+    )(hamiltonian, pattern.T, potential)
 
 
 def solution(mesh):

time: 61 us -> 47.6 us (0.78)
  Pallas kernels: 51.3 us -> 42.3 us
  local copies, waits for them, and re-layouts: 6.33 us -> 2.19 us
    pallas_call x1, Pallas kernels: 51.3 us -> 42.3 us  [local(): pl.pallas_call(functools.partial(kernel, n), out_shape=(pltpu.VMEM(hamilt...]
    unnamed x2 -> x1, local copies, waits for them, and re-layouts: 6.33 us -> 2.19 us
where the time goes in v1:
time: 47.6 us; the launch traced here: 47.4 us
  Pallas kernels  42.3 us (89%)
  between operations  2.97 us (6%)
  local copies, waits for them, and re-layouts  2.19 us (5%)
    pallas_call x1, Pallas kernels, local(): pl.pallas_call(functools.partial(kernel, n), out_shape=(pltpu.VMEM(hamilt...  42.3 us
    unnamed x1, local copies, waits for them, and re-layouts  2.19 us

profile of v1, /device:TPU:0, one launch (start us, length us, event | category | flops | bytes accessed | tf_op | source)
XLA Modules:
  0.0 47.4 jit_solution(14012494740248365744)
XLA Ops:
  1.3 42.3 %sign_iterations.1 = (f32[6,3,256,256]{3,2,1,0:T(8,128)S(1)}, f32[1]{0:T(128)}) custom-call(f32[6,3,256,256]{3,2,1,0:T(8,128)} %h.1, s32[3,96]{1,0:T(4,128)} %bitcast.1, f32[1]{0:T(128)S(6)} %copy.8.potential), custom_call_target="tpu_custom_call" | custom-call | tf_op jit(solution)/shard_map/sign_iterations/pallas_call | solution.py:269
  43.5 2.2 %copy.7 = f32[6,3,256,256]{3,2,1,0:T(8,128)} copy(f32[6,3,256,256]{3,2,1,0:T(8,128)S(1)} %get-tuple-element.2) | data formatting | bytes 9437184
